TPU v7x, 32 devices: a whole 2x2x4 slice. The times are simulated.
32 devices in a mesh: sp: 4 (over z), ctx: 4 (over y, x), fsdp: 2 (over core).
Axes of the slice: x: 2, y: 2, z: 4, core: 2. Of those that a mesh axis runs over, the one named last changes fastest.
Arguments:
- block_input: bfloat16 [2, 4, 512, 2048], P('fsdp', 'ctx', 'sp'), may hold values from -6 to 6
- cotangent: bfloat16 [2, 4, 512, 2048], P('fsdp', 'ctx', 'sp'), may hold values from -6 to 6
- decay_rate: float32 [8], replicated, may hold values from 4.8828125e-05 to 0.0333333333
- weight_in: float32 [2048, 16384], P(('sp', 'ctx', 'fsdp')), may hold values from -0.125 to 0.125
- weight_out: float32 [4096, 4096], P(('sp', 'ctx', 'fsdp')), may hold values from -0.09375 to 0.09375
- norm_gains: float32 [4, 2048], P(None, ('sp', 'ctx', 'fsdp')), may hold values from -0.9 to 1.6
- moment_in: float32 [2048, 16384], P(('sp', 'ctx', 'fsdp')), may hold values from -6 to 6
- square_in: float32 [2048, 16384], P(('sp', 'ctx', 'fsdp')), may hold values from 8.192 to 32.768
- moment_out: float32 [4096, 4096], P(('sp', 'ctx', 'fsdp')), may hold values from -6 to 6
- square_out: float32 [4096, 4096], P(('sp', 'ctx', 'fsdp')), may hold values from 8.192 to 32.768
- moment_norm: float32 [4, 2048], P(None, ('sp', 'ctx', 'fsdp')), may hold values from -6 to 6
- square_norm: float32 [4, 2048], P(None, ('sp', 'ctx', 'fsdp')), may hold values from 8.192 to 32.768
Outputs:
- block_output: bfloat16 [2, 4, 512, 2048], P('fsdp', 'ctx', 'sp')
- grad_input: bfloat16 [2, 4, 512, 2048], P('fsdp', 'ctx', 'sp')
- grad_weight_in: float32 [2048, 16384], P(('sp', 'ctx', 'fsdp'))
- new_moment_in: float32 [2048, 16384], P(('sp', 'ctx', 'fsdp'))
- new_square_in: float32 [2048, 16384], P(('sp', 'ctx', 'fsdp'))
- update_in: float32 [2048, 16384], P(('sp', 'ctx', 'fsdp'))
- grad_weight_out: float32 [4096, 4096], P(('sp', 'ctx', 'fsdp'))
- new_moment_out: float32 [4096, 4096], P(('sp', 'ctx', 'fsdp'))
- new_square_out: float32 [4096, 4096], P(('sp', 'ctx', 'fsdp'))
- update_out: float32 [4096, 4096], P(('sp', 'ctx', 'fsdp'))
- grad_norm: float32 [4, 2048], P(None, ('sp', 'ctx', 'fsdp'))
- new_moment_norm: float32 [4, 2048], P(None, ('sp', 'ctx', 'fsdp'))
- new_square_norm: float32 [4, 2048], P(None, ('sp', 'ctx', 'fsdp'))
- update_norm: float32 [4, 2048], P(None, ('sp', 'ctx', 'fsdp'))
All inputs are finite; a program needn't handle non-finite values.
Results may differ from a plain program's by a relative error of at most 0.018.
The roundings to bfloat16 on the way count: a program that leaves them out, or rounds other values in their place, can miss the bound.
Values may be sent and summed in bfloat16 or wider, within the bound.
A program may use at most 456 MiB of HBM per device.

v0:
```python
import math

import jax
import jax.numpy as jnp
from jax import lax
from jax.sharding import PartitionSpec as P

H = 8
DK = 256
DV = 512
SPAN = 512
STEP = 10
QK = 2048
VD = 4096


beta_one = 0.9
beta_two = 0.95
learn_rate = 0.01
decay_weight = 0.1
adam_eps = 1e-08
norm_eps = 1e-05
root_half = 0.7071067811865476
inv_root_tau = 0.3989422804014327


def carried_in(x, axis, combine, identity):
    count, here = (lax.axis_size(axis), lax.axis_index(axis))
    everything = jax.tree.map(lambda part: lax.all_gather(part, axis), x)
    start = jax.tree.map(
        lambda part, zero: jnp.broadcast_to(jnp.asarray(zero, part.dtype), part.shape), x, identity
    )

    def carried_hop(k, before):
        reached = k < here
        new = combine(before, jax.tree.map(lambda part: part[k], everything))
        return jax.tree.map(lambda a, b: jnp.where(reached, a, b), new, before)

    return lax.fori_loop(0, count, carried_hop, start)


def prefix(x, axis, combine, identity):
    count, here = (lax.axis_size(axis), lax.axis_index(axis))
    everything = jax.tree.map(
        lambda part, kind: lax.all_gather(part.astype(kind), axis), x, (jnp.bfloat16, jnp.bfloat16)
    )
    start = jax.tree.map(
        lambda part, zero: jnp.broadcast_to(jnp.asarray(zero, part.dtype), part.shape), x, identity
    )

    def prefix_hop(k, before):
        at = count - 1 - k
        reached = at > here
        new = combine(
            before, jax.tree.map(lambda part, own: part[at].astype(own.dtype), everything, x)
        )
        return jax.tree.map(lambda a, b: jnp.where(reached, a, b), new, before)

    return lax.fori_loop(0, count, prefix_hop, start)


def layer_stats(values, gain_row, shift_row):
    centred = values - jnp.mean(values, axis=-1, keepdims=True)
    inv_std = lax.rsqrt(jnp.mean(centred * centred, axis=-1, keepdims=True) + norm_eps)
    unit_vals = centred * inv_std
    return (unit_vals * gain_row + shift_row, unit_vals, inv_std)


def layer_back(grad_vals, unit_vals, inv_std, gain_row):
    scaled = grad_vals * gain_row
    return inv_std * (
        scaled
        - jnp.mean(scaled, axis=-1, keepdims=True)
        - unit_vals * jnp.mean(scaled * unit_vals, axis=-1, keepdims=True)
    )


def angles(positions, head_size):
    half_size = head_size // 2
    inverse = jnp.exp(
        -math.log(10000.0) * (2.0 * jnp.arange(half_size, dtype=jnp.float32) / head_size)
    )
    phases = positions.astype(jnp.float32)[:, None] * inverse[None, :]
    return (jnp.cos(phases)[:, None, :], jnp.sin(phases)[:, None, :])


def rotate(values, cosine, sine, sign_flip):
    half_size = values.shape[-1] // 2
    first_half = values[..., :half_size]
    second_half = values[..., half_size:]
    return jnp.concatenate(
        [
            first_half * cosine - sign_flip * (second_half * sine),
            second_half * cosine + sign_flip * (first_half * sine),
        ],
        -1,
    )


def chain(earlier, latter):
    return (earlier[0] * latter[1][:, None, None] + latter[0], earlier[1] * latter[1])


def adam_update(weight, grad_vals, moment, square):
    moment_new = beta_one * moment + (1.0 - beta_one) * grad_vals
    square_new = beta_two * square + (1.0 - beta_two) * grad_vals * grad_vals
    moment_hat = moment_new / (1.0 - beta_one**STEP)
    square_hat = square_new / (1.0 - beta_two**STEP)
    step_vals = -learn_rate * (
        moment_hat / (jnp.sqrt(square_hat) + adam_eps) + decay_weight * weight
    )
    return (moment_new, square_new, step_vals)


def shards(
    block_input,
    cotangent,
    decay_rate,
    weight_in,
    weight_out,
    norm_gains,
    moment_in,
    square_in,
    moment_out,
    square_out,
    moment_norm,
    square_norm,
):
    tok_count = block_input.shape[2]
    model_width = block_input.shape[3]
    sp_count = lax.axis_size("sp")
    heads_dev = H // sp_count
    block_len = tok_count * sp_count
    sp_index = lax.axis_index("sp")
    ctx_index = lax.axis_index("ctx")
    cut_at = 2 * QK + 2 * VD
    last_last = (((1,), (1,)), ((), ()))
    first_first = (((0,), (0,)), ((), ()))
    local_weights = (
        weight_in.astype(jnp.bfloat16),
        weight_out.astype(jnp.bfloat16),
        norm_gains.astype(jnp.bfloat16),
    )
    full_in, full_out, full_norms = (
        lax.all_gather(local_weights[0], ("sp", "ctx", "fsdp"), axis=0, tiled=True),
        lax.all_gather(local_weights[1], ("sp", "ctx", "fsdp"), axis=0, tiled=True),
        lax.all_gather(local_weights[2], ("sp", "ctx", "fsdp"), axis=1, tiled=True),
    )
    gains = full_norms.astype(jnp.float32)
    row_vals = block_input.reshape(tok_count, model_width).astype(jnp.float32)
    normed_a, unit_a, scale_a = layer_stats(row_vals, gains[0], gains[1])
    a_low = normed_a.astype(jnp.bfloat16)
    projected = jnp.dot(a_low, full_in[:, :cut_at], preferred_element_type=jnp.float32)
    token_pos = (
        ctx_index * block_len + sp_index * tok_count + jnp.arange(tok_count, dtype=jnp.int32)
    )
    cos_tok, sin_tok = angles(token_pos, DK)
    query_low = rotate(projected[:, :QK].reshape(tok_count, H, DK), cos_tok, sin_tok, 1.0).astype(
        jnp.bfloat16
    )
    key_low = rotate(
        projected[:, QK : 2 * QK].reshape(tok_count, H, DK), cos_tok, sin_tok, 1.0
    ).astype(jnp.bfloat16)
    value_low = projected[:, 2 * QK : 2 * QK + VD].reshape(tok_count, H, DV).astype(jnp.bfloat16)
    gate_pre = projected[:, 2 * QK + VD :]
    q_head, k_head, v_head = (
        lax.all_to_all(query_low, "sp", split_axis=1, concat_axis=0, tiled=True),
        lax.all_to_all(key_low, "sp", split_axis=1, concat_axis=0, tiled=True),
        lax.all_to_all(value_low, "sp", split_axis=1, concat_axis=0, tiled=True),
    )
    rates = lax.dynamic_slice_in_dim(decay_rate, sp_index * heads_dev, heads_dev)
    span_count = block_len // SPAN
    offsets = jnp.arange(SPAN, dtype=jnp.float32)
    spacing = offsets[:, None] - offsets[None, :]
    decay_mask = jnp.where(
        spacing[None] >= 0.0, jnp.exp(-rates[:, None, None] * jnp.maximum(spacing, 0.0)[None]), 0.0
    )
    inward = jnp.exp(-rates[None, :] * (offsets[:, None] + 1.0))
    target_dtype_cast = jnp.exp(-rates[None, :] * (SPAN - 1.0 - offsets[:, None]))
    span_fall = jnp.exp(-rates * SPAN)
    block_fall = jnp.exp(-rates * block_len)
    query_shard_pieces = q_head.reshape(span_count, SPAN, heads_dev, DK)
    k_parts = k_head.reshape(span_count, SPAN, heads_dev, DK)
    value_shard_pieces = v_head.reshape(span_count, SPAN, heads_dev, DV)
    key_decayed = (k_parts * target_dtype_cast[None, :, :, None]).astype(jnp.bfloat16)
    updates = jnp.einsum(
        "cjhk,cjhv->chkv", key_decayed, value_shard_pieces, preferred_element_type=jnp.float32
    )
    span_steps = jnp.arange(span_count, dtype=jnp.float32)
    own_falls = jnp.exp(-rates[None, :] * (SPAN * (span_count - 1.0 - span_steps))[:, None])
    own_state = jnp.sum(updates * own_falls[:, :, None, None], 0)
    identity = (jnp.zeros_like(own_state), jnp.ones_like(block_fall))
    incoming, _ = carried_in((own_state, block_fall), "ctx", chain, identity)
    state_reduced = [incoming.astype(jnp.bfloat16)]
    shard_span_slice = 0
    scores = jnp.einsum(
        "ihk,jhk->hij",
        query_shard_pieces[shard_span_slice],
        k_parts[shard_span_slice],
        preferred_element_type=jnp.float32,
    )
    prob_low = (scores * decay_mask).astype(jnp.bfloat16)
    inner_sum = jnp.einsum(
        "hij,jhv->ihv",
        prob_low,
        value_shard_pieces[shard_span_slice],
        preferred_element_type=jnp.float32,
    )
    readout_total = jnp.einsum(
        "map,apn->man",
        query_shard_pieces[shard_span_slice],
        state_reduced[shard_span_slice],
        preferred_element_type=jnp.float32,
    )
    out_pieces = (inner_sum + readout_total * inward[:, :, None]).astype(jnp.bfloat16)
    mixed = lax.all_to_all(out_pieces, "sp", split_axis=0, concat_axis=1, tiled=True)
    mixed_vals = mixed.astype(jnp.float32)
    centred = mixed_vals - jnp.mean(mixed_vals, axis=-1, keepdims=True)
    group_scale = lax.rsqrt(jnp.mean(centred * centred, axis=-1, keepdims=True) + norm_eps)
    unit_heads = centred * group_scale
    unit_flat = unit_heads.reshape(tok_count, VD)
    gate_sig = jax.nn.sigmoid(gate_pre)
    gate_act = gate_pre * gate_sig
    gated = (gate_act * unit_flat).astype(jnp.bfloat16)
    branch = jnp.dot(gated, full_out[:, :model_width], preferred_element_type=jnp.float32)
    hidden = row_vals + branch
    normed_b, unit_b, scale_b = layer_stats(hidden, gains[2], gains[3])
    b_low = normed_b.astype(jnp.bfloat16)
    up_proj = jnp.dot(b_low, full_in[:, cut_at:], preferred_element_type=jnp.float32)
    act_low = jax.nn.gelu(up_proj, approximate=False).astype(jnp.bfloat16)
    ffn_out = jnp.dot(act_low, full_out[:, model_width:], preferred_element_type=jnp.float32)
    block_out = (hidden + ffn_out).astype(jnp.bfloat16).reshape(block_input.shape)
    full_in, full_out, full_norms = (
        lax.all_gather(local_weights[0], ("sp", "ctx", "fsdp"), axis=0, tiled=True),
        lax.all_gather(local_weights[1], ("sp", "ctx", "fsdp"), axis=0, tiled=True),
        lax.all_gather(local_weights[2], ("sp", "ctx", "fsdp"), axis=1, tiled=True),
    )
    grad_top = cotangent.reshape(tok_count, model_width).astype(jnp.float32)
    grad_ffn = grad_top.astype(jnp.bfloat16)
    grad_act = lax.dot_general(
        grad_ffn, full_out[:, model_width:], last_last, preferred_element_type=jnp.float32
    )
    density = (
        0.5 * (1.0 + lax.erf(up_proj * root_half))
        + up_proj * jnp.exp(-0.5 * up_proj * up_proj) * inv_root_tau
    )
    grad_up = (grad_act * density).astype(jnp.bfloat16)
    grad_b = lax.dot_general(
        grad_up, full_in[:, cut_at:], last_last, preferred_element_type=jnp.float32
    )
    grad_hidden = grad_top + layer_back(grad_b, unit_b, scale_b, gains[2])
    grad_branch = grad_hidden.astype(jnp.bfloat16)
    grad_gated = lax.dot_general(
        grad_branch, full_out[:, :model_width], last_last, preferred_element_type=jnp.float32
    )
    grad_gate = (grad_gated * unit_flat * gate_sig * (1.0 + gate_pre * (1.0 - gate_sig))).astype(
        jnp.bfloat16
    )
    grad_unit = (grad_gated * gate_act).reshape(tok_count, H, DV)
    grad_mixed = (
        group_scale
        * (
            grad_unit
            - jnp.mean(grad_unit, axis=-1, keepdims=True)
            - unit_heads * jnp.mean(grad_unit * unit_heads, axis=-1, keepdims=True)
        )
    ).astype(jnp.bfloat16)
    grad_head = lax.all_to_all(grad_mixed, "sp", split_axis=1, concat_axis=0, tiled=True)
    g_parts = grad_head.reshape(span_count, SPAN, heads_dev, DV)
    shard_span_slice = 0
    gradient_readout = (g_parts[shard_span_slice] * inward[:, :, None]).astype(jnp.bfloat16)
    read_grads = [gradient_readout]
    reach_now = jnp.einsum(
        "mqo,mqd->qod",
        query_shard_pieces[shard_span_slice],
        gradient_readout,
        preferred_element_type=jnp.float32,
    )
    reach = [reach_now]
    own_grad = reach_now * jnp.exp(-rates * (SPAN * float(shard_span_slice)))[:, None, None]
    later_grad, _ = prefix((own_grad, block_fall), "ctx", chain, identity)
    grad_qs = [None] * span_count
    grad_ks = [None] * span_count
    grad_vs = [None] * span_count
    carried = later_grad
    for shard_span_slice in reversed(range(span_count)):
        carried_state_reduced = carried.astype(jnp.bfloat16)
        scores = jnp.einsum(
            "ihk,jhk->hij",
            query_shard_pieces[shard_span_slice],
            k_parts[shard_span_slice],
            preferred_element_type=jnp.float32,
        )
        prob_low = (scores * decay_mask).astype(jnp.bfloat16)
        grad_probs = jnp.einsum(
            "ihv,jhv->hij",
            g_parts[shard_span_slice],
            value_shard_pieces[shard_span_slice],
            preferred_element_type=jnp.float32,
        )
        grad_scores = (grad_probs * decay_mask).astype(jnp.bfloat16)
        grad_q = jnp.einsum(
            "hij,jhk->ihk",
            grad_scores,
            k_parts[shard_span_slice],
            preferred_element_type=jnp.float32,
        )
        grad_q = grad_q + jnp.einsum(
            "qxr,xgr->qxg",
            read_grads[shard_span_slice],
            state_reduced[shard_span_slice],
            preferred_element_type=jnp.float32,
        )
        grad_k = jnp.einsum(
            "hij,ihk->jhk",
            grad_scores,
            query_shard_pieces[shard_span_slice],
            preferred_element_type=jnp.float32,
        )
        grad_kw = jnp.einsum(
            "xma,mua->xmu",
            value_shard_pieces[shard_span_slice],
            carried_state_reduced,
            preferred_element_type=jnp.float32,
        )
        grad_k = grad_k + grad_kw * target_dtype_cast[:, :, None]
        grad_v = jnp.einsum(
            "hij,ihv->jhv", prob_low, g_parts[shard_span_slice], preferred_element_type=jnp.float32
        )
        grad_v = grad_v + jnp.einsum(
            "rnd,ndt->rnt",
            key_decayed[shard_span_slice],
            carried_state_reduced,
            preferred_element_type=jnp.float32,
        )
        grad_qs[shard_span_slice] = grad_q
        grad_ks[shard_span_slice] = grad_k
        grad_vs[shard_span_slice] = grad_v
        carried = span_fall[:, None, None] * carried + reach[shard_span_slice]
    head_pos = ctx_index * block_len + jnp.arange(block_len, dtype=jnp.int32)
    cos_head, sin_head = angles(head_pos, DK)
    back_q = rotate(grad_qs[0], cos_head, sin_head, -1.0).astype(jnp.bfloat16)
    back_k = rotate(grad_ks[0], cos_head, sin_head, -1.0).astype(jnp.bfloat16)
    back_v = grad_vs[0].astype(jnp.bfloat16)
    tok_q, tok_k, tok_v = (
        lax.all_to_all(back_q, "sp", split_axis=0, concat_axis=1, tiled=True),
        lax.all_to_all(back_k, "sp", split_axis=0, concat_axis=1, tiled=True),
        lax.all_to_all(back_v, "sp", split_axis=0, concat_axis=1, tiled=True),
    )
    grad_proj = jnp.concatenate(
        [
            tok_q.reshape(tok_count, QK),
            tok_k.reshape(tok_count, QK),
            tok_v.reshape(tok_count, VD),
            grad_gate,
        ],
        1,
    )
    grad_a = lax.dot_general(
        grad_proj, full_in[:, :cut_at], last_last, preferred_element_type=jnp.float32
    )
    grad_rows = grad_hidden + layer_back(grad_a, unit_a, scale_a, gains[0])
    grad_x = grad_rows.astype(jnp.bfloat16).reshape(block_input.shape)
    norm_terms = jnp.stack(
        [
            jnp.sum(grad_a * unit_a, 0),
            jnp.sum(grad_a, 0),
            jnp.sum(grad_b * unit_b, 0),
            jnp.sum(grad_b, 0),
        ]
    )
    grad_gains = lax.psum_scatter(
        norm_terms, ("sp", "ctx", "fsdp"), scatter_dimension=1, tiled=True
    )
    grad_first = lax.psum_scatter(
        jnp.concatenate(
            [
                lax.dot_general(a_low, grad_proj, first_first, preferred_element_type=jnp.float32),
                lax.dot_general(b_low, grad_up, first_first, preferred_element_type=jnp.float32),
            ],
            1,
        ),
        ("sp", "ctx", "fsdp"),
        scatter_dimension=0,
        tiled=True,
    )
    grad_second = lax.psum_scatter(
        jnp.concatenate(
            [
                lax.dot_general(
                    gated, grad_branch, first_first, preferred_element_type=jnp.float32
                ),
                lax.dot_general(act_low, grad_ffn, first_first, preferred_element_type=jnp.float32),
            ],
            1,
        ),
        ("sp", "ctx", "fsdp"),
        scatter_dimension=0,
        tiled=True,
    )
    first_m, first_v, first_step = adam_update(weight_in, grad_first, moment_in, square_in)
    second_m, second_v, second_step = adam_update(weight_out, grad_second, moment_out, square_out)
    gain_m, gain_v, gain_step = adam_update(norm_gains, grad_gains, moment_norm, square_norm)
    return (
        block_out,
        grad_x,
        grad_first,
        first_m,
        first_v,
        first_step,
        grad_second,
        second_m,
        second_v,
        second_step,
        grad_gains,
        gain_m,
        gain_v,
        gain_step,
    )


def solution(mesh):
    in_specs = (
        P("fsdp", "ctx", "sp", None),
        P("fsdp", "ctx", "sp", None),
        P(),
        P(("sp", "ctx", "fsdp"), None),
        P(("sp", "ctx", "fsdp"), None),
        P(None, ("sp", "ctx", "fsdp")),
        P(("sp", "ctx", "fsdp"), None),
        P(("sp", "ctx", "fsdp"), None),
        P(("sp", "ctx", "fsdp"), None),
        P(("sp", "ctx", "fsdp"), None),
        P(None, ("sp", "ctx", "fsdp")),
        P(None, ("sp", "ctx", "fsdp")),
    )
    out_specs = (
        P("fsdp", "ctx", "sp", None),
        P("fsdp", "ctx", "sp", None),
        P(("sp", "ctx", "fsdp"), None),
        P(("sp", "ctx", "fsdp"), None),
        P(("sp", "ctx", "fsdp"), None),
        P(("sp", "ctx", "fsdp"), None),
        P(("sp", "ctx", "fsdp"), None),
        P(("sp", "ctx", "fsdp"), None),
        P(("sp", "ctx", "fsdp"), None),
        P(("sp", "ctx", "fsdp"), None),
        P(None, ("sp", "ctx", "fsdp")),
        P(None, ("sp", "ctx", "fsdp")),
        P(None, ("sp", "ctx", "fsdp")),
        P(None, ("sp", "ctx", "fsdp")),
    )
    return jax.shard_map(shards, mesh=mesh, in_specs=in_specs, out_specs=out_specs, check_vma=False)
```

profile of v0, /device:TPU:0, one launch (start us, length us, event | category | flops | bytes accessed | tf_op | source)
XLA Modules:
  0.0 3226.5 jit_solution(14098670158303530982)
XLA Ops:
  11.6 44.7 %all-gather.4 = bf16[32,64,4]{1,2,0:T(4,128)(2,1)S(1)} all-gather(bf16[1,64,4]{1,2,0:T(4,128)(2,1)S(1)} %convert_bitcast_fusion.2), channel_id=1, replica_groups=mesh['sp'=4,'ctx'=4,'fsdp'=2] {'sp','ctx','fsdp'}, dimensions={0}, use_global_device_ids=true | all-gather | bytes 16896 | tf_op jit(solution)/shard_map/all_gather | solution.py:147
  57.3 312.5 %all-gather.10.cloned.1.call-done = bf16[2048,16384]{1,0:T(8,128)(2,1)} async-done(((bf16[64,16384]{1,0:T(8,128)(2,1)}), bf16[2048,16384]{1,0:T(8,128)(2,1)}) %all-gather.10.cloned.1.call-update) | async-done | bytes 67108880 | tf_op jit(solution)/shard_map/all_gather | solution.py:145
  369.9 20.2 fusion.4
  400.1 12.4 all-to-all-done.2
  417.7 23.9 all-to-all-done
  453.4 9.4 all-reduce
  472.6 24.5 all-gather.14.cloned.1.call-done
  497.2 6.7 while.30
  509.0 49.9 %all_to_all.126 = bf16[512,2,512]{2,1,0:T(2,128)(2,1)S(1)} all-to-all(bf16[512,2,512]{2,1,0:T(2,128)(2,1)S(1)} %copy.252), channel_id=1, replica_groups=mesh['sp'=4,'ctx'=4,'fsdp'=2] {'sp'}, dimensions={0} | all-to-all | bytes 2097152 | tf_op jit(solution)/shard_map/all_to_all | solution.py:216
  581.6 134.4 %all-gather.12.cloned.1.call-done = bf16[4096,4096]{1,0:T(8,128)(2,1)} async-done(((bf16[128,4096]{1,0:T(8,128)(2,1)}), bf16[4096,4096]{1,0:T(8,128)(2,1)}) %all-gather.12.cloned.1.call-update) | async-done | bytes 33554448 | tf_op jit(solution)/shard_map/all_gather | solution.py:146
  716.0 8.5 fusion.115
  724.9 7.3 fusion.12
  733.5 10.3 fusion.21
  743.8 12.8 multiply_reduce_fusion.1
  759.9 12.2 fusion.96
  780.3 28.8 all_to_all.127
  813.4 9.0 all-reduce.1
  829.9 16.7 all-gather.16.cloned.1.call-done
  864.2 12.1 all-to-all-done.6
  884.3 10.2 all-to-all-done.5
  898.1 15.6 fusion.86
  913.7 13.1 fusion.91
  933.8 24.7 fusion.79
  960.0 44.5 %pad_maximum_fusion.1 = f32[4096,4096]{0,1:T(8,128)} fusion(f32[4096,2048]{0,1:T(8,128)} %fusion.86, f32[4096,2048]{0,1:T(8,128)} %fusion.91), kind=kLoop, calls=%fused_computation.7 | loop fusion | flops 16777216 | bytes 134217728 | tf_op jit(solution)/shard_map/concatenate | solution.py:388
  1005.7 14.6 fusion.104
  1020.3 36.1 %fusion.84 = f32[2048,12288]{1,0:T(8,128)} fusion(bf16[128,4096]{1,0:T(8,128)(2,1)} %get-tuple-element.402, bf16[128,4096]{1,0:T(8,128)(2,1)S(1)} %reshape.429, bf16[128,2048]{1,0:T(8,128)(2,1)S(1)} %copy-done.30, bf16[128,2048]{1,0:T(8,128)(2,1)} %reshape.427, bf16[1,1,128,2048]{3,2,1,0:T(8,128)(2,1)S(1)} %copy-done.15, f32[2048]{0:T(1024)S(1)} %bitcast.248, ...), kind=kOutput, calls=%fused_computation.130 | convolution fusion | flops 6456606720 | bytes 104350720 | tf_op jit(solution)/shard_map/dot_general | solution.py:378
  1056.4 88.2 %pad_maximum_fusion = f32[2048,16384]{1,0:T(8,128)} fusion(f32[2048,4096]{1,0:T(8,128)} %fusion.104, f32[2048,12288]{1,0:T(8,128)} %fusion.84), kind=kLoop, calls=%fused_computation.6 | loop fusion | flops 33554432 | bytes 268435456 | tf_op jit(solution)/shard_map/concatenate | solution.py:376
  1153.3 11.7 fusion.34
  1167.9 629.9 %reduce-scatter.9.cloned.1.call-done = f32[128,4096]{0,1:T(8,128)} async-done(((f32[4096,4096]{0,1:T(8,128)}), f32[128,4096]{0,1:T(8,128)}) %reduce-scatter.9.cloned.1.call-update) | async-done | bytes 2097168 | tf_op jit(solution)/shard_map/reduce_scatter | solution.py:387
  1797.8 7.0 add_multiply_fusion.1
  1814.3 1393.4 %reduce-scatter.13.cloned.1.call-done = f32[64,16384]{1,0:T(8,128)} async-done(((f32[2048,16384]{1,0:T(8,128)}), f32[64,16384]{1,0:T(8,128)}) %reduce-scatter.13.cloned.1.call-update) | async-done | bytes 4194320
  3207.7 11.5 add_multiply_fusion
  (273 shorter events, 165.7 us)
Async XLA Ops:
  7.2 362.7 %all-gather.10.cloned.1.call-start = ((), (), s32[]{:S(2)}) async-start(), calls=%async_computation.11 | async-start | bytes 69206016 | tf_op jit(solution)/shard_map/all_gather | solution.py:145
  10.9 45.5 %copy-start.14 = (bf16[1,1,128,2048]{3,2,1,0:T(8,128)(2,1)S(1)}, bf16[1,1,128,2048]{3,2,1,0:T(8,128)(2,1)}, u32[]{:S(2)}) copy-start(bf16[1,1,128,2048]{3,2,1,0:T(8,128)(2,1)} %param.16) | copy-start | bytes 1572868
  57.3 332.8 %copy-start.35 = (f32[1,2048]{1,0:T(1,128)}, f32[1,2048]{1,0:T(1,128)S(1)}, u32[]{:S(2)}) copy-start(f32[1,2048]{1,0:T(1,128)S(1)} %get-tuple-element.423) | copy-start | bytes 24580
  57.3 667.5 %copy-start.42 = (f32[1,2048]{1,0:T(1,128)}, f32[1,2048]{1,0:T(1,128)S(1)}, u32[]{:S(2)}) copy-start(f32[1,2048]{1,0:T(1,128)S(1)} %get-tuple-element.422) | copy-start | bytes 24580
  57.3 700.5 %copy-start.40 = (f32[1,2048]{1,0:T(1,128)}, f32[1,2048]{1,0:T(1,128)S(1)}, u32[]{:S(2)}) copy-start(f32[1,2048]{1,0:T(1,128)S(1)} %get-tuple-element.421) | copy-start | bytes 24580
  393.9 18.6 all-to-all-start.2
  399.1 17.0 copy-start.54
  399.1 18.3 copy-start.53
  412.5 29.1 all-to-all-start
  416.0 81.1 %all-gather.14.cloned.1.call-start = ((), (), s32[]{:S(2)}) async-start(), calls=%async_computation.14 | async-start | bytes 5242880 | tf_op jit(solution)/shard_map/all_gather | solution.py:29
  417.7 49.7 %copy-start.22 = (bf16[128,4,2,256]{3,0,1,2:T(8,128)(2,1)}, bf16[128,4,2,256]{3,0,1,2:T(8,128)(2,1)S(1)}, u32[]{:S(2)}) copy-start(bf16[128,4,2,256]{3,0,1,2:T(8,128)(2,1)S(1)} %copy.248) | copy-start | bytes 1572868
  444.5 25.1 copy-start.3
  446.2 269.8 %all-gather.12.cloned.1.call-start = ((), (), s32[]{:S(2)}) async-start(), calls=%async_computation.12 | async-start | bytes 34603008 | tf_op jit(solution)/shard_map/all_gather | solution.py:146
  449.8 17.5 all-to-all-start.1
  453.3 393.3 %all-gather.16.cloned.1.call-start = ((), (), s32[]{:S(2)}) async-start(), calls=%async_computation.15 | async-start | bytes 2621440 | tf_op jit(solution)/shard_map/all_gather | solution.py:45
  724.5 19.3 copy-start.5
  724.6 33.3 %copy-start.44 = (f32[128]{0:T(128)}, f32[128]{0:T(128)S(1)}, u32[]{:S(2)}) copy-start(f32[128]{0:T(128)S(1)} %broadcast_multiply_fusion.7) | copy-start | bytes 1540
  724.8 33.0 %copy-start.46 = (f32[128]{0:T(128)}, f32[128]{0:T(128)S(1)}, u32[]{:S(2)}) copy-start(f32[128]{0:T(128)S(1)} %add_rsqrt_fusion.1) | copy-start | bytes 1540
  759.9 12.3 copy-start.8
  810.3 13.9 copy-start.4
  857.1 23.3 copy-start.13
  857.1 23.3 copy-start.29
  857.1 19.2 all-to-all-start.6
  876.3 18.3 all-to-all-start.5
  894.5 37.5 %all-to-all-start.7 = ((bf16[512,2,512]{2,1,0:T(2,128)(2,1)}), bf16[512,2,512]{2,1,0:T(2,128)(2,1)S(1)}, u32[]{:S(2)}, u32[]{:S(2)}) async-start(bf16[512,2,512]{2,1,0:T(2,128)(2,1)} %copy.283), calls=%async_computation.7 | async-start | bytes 2097152 | tf_op jit(solution)/shard_map/all_to_all | solution.py:348
  898.1 15.7 copy-start.9
  898.1 15.6 copy-start.25
  898.1 268.4 %reduce-scatter.11.cloned.1.call-start = ((), (), s32[]{:S(2)}) async-start(), calls=%async_computation.16 | async-start | bytes 1081344
  959.9 837.9 %reduce-scatter.9.cloned.1.call-start = ((), (), s32[]{:S(2)}) async-start(), calls=%async_computation.13 | async-start | bytes 69206016 | tf_op jit(solution)/shard_map/reduce_scatter | solution.py:387
  1004.5 15.8 copy-start.36
  1004.5 2203.2 %reduce-scatter.13.cloned.1.call-start = ((), (), s32[]{:S(2)}) async-start(), calls=%async_computation.17 | async-start | bytes 138412032
  1167.3 637.5 %copy-start.48 = (f32[4,64]{1,0:T(4,128)}, f32[4,64]{1,0:T(4,128)S(1)}, u32[]{:S(2)}) copy-start(f32[4,64]{1,0:T(4,128)S(1)} %copy.310) | copy-start | bytes 3076
  (39 other events, 138.2 us)
Sparse Core Ops, SparseCore 0:
  11.4 358.4 all-gather.9
  446.3 50.7 all-gather.13
  500.6 215.3 all-gather.11
  813.3 33.3 all-gather.15
  960.1 136.9 reduce-scatter.10
  1099.2 698.5 reduce-scatter.8
  1800.7 1406.9 reduce-scatter.12
where the time goes:
time: 3240 us; the launch traced here: 3230 us
  waiting for transfers between devices  2570 us (79%)
  matrix products  207 us (6%)
  other arithmetic  196 us (6%)
  blocking collectives  142 us (4%)
  local copies, waits for them, and re-layouts  68.6 us (2%)
    unnamed x9, waiting for transfers between devices  1390 us
    reduce_scatter x1, waiting for transfers between devices, shards(): lax.psum_scatter(jnp.concatenate([lax.dot_general(gated, grad_branch, fir...  630 us
    all_gather x1, waiting for transfers between devices, shards(): lax.all_gather(local_weights[0], ('sp', 'ctx', 'fsdp'), axis=0, tiled=True)  313 us
    all_gather x1, waiting for transfers between devices, shards(): lax.all_gather(local_weights[1], ('sp', 'ctx', 'fsdp'), axis=0, tiled=True)  134 us
    concatenate x1, other arithmetic, shards(): jnp.concatenate([lax.dot_general(a_low, grad_proj, first_first, preferred...  88.2 us
  transfers between devices with their start and end apart: 13, of which 11 were waited for; matrix products, arithmetic and copies ran while one was open for 10% of the time, Pallas kernels for 0%

commit v1 on v0

v1 whole, which is shorter than its diff:
```python
import math

import jax
import jax.numpy as jnp
from jax import lax
from jax.sharding import PartitionSpec as P

H = 8
DK = 256
DV = 512
SPAN = 512
STEP = 10
QK = 2048
VD = 4096

beta_one = 0.9
beta_two = 0.95
learn_rate = 0.01
decay_weight = 0.1
adam_eps = 1e-08
norm_eps = 1e-05
root_half = 0.7071067811865476
inv_root_tau = 0.3989422804014327

BF = jnp.bfloat16
F32 = jnp.float32
ALL = ("sp", "ctx", "fsdp")
PLANE = ("ctx", "fsdp")


def layer_stats(values, gain_row, shift_row):
    centred = values - jnp.mean(values, axis=-1, keepdims=True)
    inv_std = lax.rsqrt(jnp.mean(centred * centred, axis=-1, keepdims=True) + norm_eps)
    unit_vals = centred * inv_std
    return (unit_vals * gain_row + shift_row, unit_vals, inv_std)


def layer_back(grad_vals, unit_vals, inv_std, gain_row):
    scaled = grad_vals * gain_row
    return inv_std * (
        scaled
        - jnp.mean(scaled, axis=-1, keepdims=True)
        - unit_vals * jnp.mean(scaled * unit_vals, axis=-1, keepdims=True)
    )


def angles(positions, head_size):
    half_size = head_size // 2
    inverse = jnp.exp(
        -math.log(10000.0) * (2.0 * jnp.arange(half_size, dtype=jnp.float32) / head_size)
    )
    phases = positions.astype(jnp.float32)[:, None] * inverse[None, :]
    return (jnp.cos(phases), jnp.sin(phases))


def rotate(values, cosine, sine, sign_flip):
    half_size = values.shape[-1] // 2
    first_half = values[..., :half_size]
    second_half = values[..., half_size:]
    return jnp.concatenate(
        [
            first_half * cosine - sign_flip * (second_half * sine),
            second_half * cosine + sign_flip * (first_half * sine),
        ],
        -1,
    )


def adam_update(weight, grad_vals, moment, square):
    moment_new = beta_one * moment + (1.0 - beta_one) * grad_vals
    square_new = beta_two * square + (1.0 - beta_two) * grad_vals * grad_vals
    moment_hat = moment_new / (1.0 - beta_one**STEP)
    square_hat = square_new / (1.0 - beta_two**STEP)
    step_vals = -learn_rate * (
        moment_hat / (jnp.sqrt(square_hat) + adam_eps) + decay_weight * weight
    )
    return (moment_new, square_new, step_vals)


def mm(a, b):
    return jnp.dot(a, b, preferred_element_type=F32)


def mm_t(a, b):
    return lax.dot_general(a, b, (((1,), (1,)), ((), ())), preferred_element_type=F32)


def mm_tn(a, b):
    return lax.dot_general(a, b, (((0,), (0,)), ((), ())), preferred_element_type=F32)


def ein(spec, a, b):
    return jnp.einsum(spec, a, b, preferred_element_type=F32)


def shards(
    block_input,
    cotangent,
    decay_rate,
    weight_in,
    weight_out,
    norm_gains,
    moment_in,
    square_in,
    moment_out,
    square_out,
    moment_norm,
    square_norm,
):
    tok_count = block_input.shape[2]
    width = block_input.shape[3]
    sp_n = lax.axis_size("sp")
    ctx_n = lax.axis_size("ctx")
    plane_n = ctx_n * lax.axis_size("fsdp")
    heads = H // sp_n
    block_len = tok_count * sp_n
    sp_i = lax.axis_index("sp")
    ctx_i = lax.axis_index("ctx")
    rows_in = weight_in.shape[0]
    qk_w, vd_w = QK // sp_n, VD // sp_n
    widths = (qk_w, qk_w, vd_w, vd_w, vd_w)
    starts = (0, QK, 2 * QK, 2 * QK + VD, 2 * QK + 2 * VD)
    cut = 2 * qk_w + 2 * vd_w

    def perm(v):
        return v.reshape(-1, sp_n, plane_n, rows_in).swapaxes(1, 2).reshape(v.shape)

    def unperm(v):
        return v.reshape(-1, plane_n, sp_n, rows_in).swapaxes(1, 2).reshape(v.shape)

    w_low = weight_in.astype(BF)
    slabs = jnp.concatenate(
        [w_low[:, o : o + sp_n * w].reshape(rows_in, sp_n, w) for o, w in zip(starts, widths)], 2
    )
    turned = lax.all_to_all(slabs.swapaxes(0, 1), "sp", split_axis=0, concat_axis=0, tiled=True)
    turned = turned.reshape(sp_n * rows_in, -1)
    w_proj = lax.all_gather(turned[:, :cut], PLANE, axis=0, tiled=True)
    w_up = lax.all_gather(turned[:, cut:], PLANE, axis=0, tiled=True)
    o_low = weight_out.astype(BF)
    w_o = lax.all_gather(o_low[:, :width], PLANE, axis=0, tiled=True)
    w_down = lax.all_gather(o_low[:, width:], PLANE, axis=0, tiled=True)
    gains = lax.all_gather(norm_gains.astype(BF), ALL, axis=1, tiled=True).astype(F32)
    gains_p = perm(gains)

    own_x = block_input.reshape(tok_count, width)
    own_xp = perm(own_x)
    grad_ffn_own = cotangent.reshape(tok_count, width)
    full_x = lax.all_gather(own_xp, "sp", axis=0, tiled=True).astype(F32)
    grad_ffn = lax.all_gather(grad_ffn_own, "sp", axis=0, tiled=True)
    normed_a, _, _ = layer_stats(full_x, gains_p[0], gains_p[1])
    a_low = normed_a.astype(BF)
    proj = mm(a_low, w_proj)
    head_pos = ctx_i * block_len + jnp.arange(block_len, dtype=jnp.int32)
    cos_h, sin_h = angles(head_pos, DK)

    def split_heads(v, size):
        return v.reshape(block_len, heads, size).swapaxes(0, 1)

    def join_heads(v):
        return v.swapaxes(0, 1).reshape(block_len, -1)

    qs = rotate(split_heads(proj[:, :qk_w], DK), cos_h, sin_h, 1.0).astype(BF)
    ks = rotate(split_heads(proj[:, qk_w : 2 * qk_w], DK), cos_h, sin_h, 1.0).astype(BF)
    vs = split_heads(proj[:, 2 * qk_w : 2 * qk_w + vd_w], DV).astype(BF)
    gate = split_heads(proj[:, 2 * qk_w + vd_w :], DV)

    rates = lax.dynamic_slice_in_dim(decay_rate, sp_i * heads, heads)
    offs = jnp.arange(block_len, dtype=F32)
    spacing = offs[:, None] - offs[None, :]
    mask = jnp.where(
        spacing[None] >= 0.0, jnp.exp(-rates[:, None, None] * jnp.maximum(spacing, 0.0)[None]), 0.0
    )
    inward = jnp.exp(-rates[:, None] * (offs[None, :] + 1.0))[:, :, None]
    outward = jnp.exp(-rates[:, None] * (block_len - 1.0 - offs[None, :]))[:, :, None]
    blocks = jnp.arange(ctx_n)
    back_gap = (ctx_i - 1 - blocks).astype(F32)
    back_w = jnp.where(
        blocks[:, None] < ctx_i,
        jnp.exp(-rates[None, :] * block_len * jnp.maximum(back_gap, 0.0)[:, None]),
        0.0,
    )
    fore_gap = (blocks - ctx_i - 1).astype(F32)
    fore_w = jnp.where(
        blocks[:, None] > ctx_i,
        jnp.exp(-rates[None, :] * block_len * jnp.maximum(fore_gap, 0.0)[:, None]),
        0.0,
    )

    key_decayed = (ks * outward).astype(BF)
    own_state = ein("hjk,hjv->hkv", key_decayed, vs)
    states = lax.all_gather(own_state.astype(BF), "ctx").astype(F32)
    state = jnp.sum(states * back_w[:, :, None, None], 0).astype(BF)
    scores = ein("hik,hjk->hij", qs, ks)
    probs = (scores * mask).astype(BF)
    mixed = (ein("hij,hjv->hiv", probs, vs) + ein("hik,hkv->hiv", qs, state) * inward).astype(BF)
    mixed_vals = mixed.astype(F32)
    centred = mixed_vals - jnp.mean(mixed_vals, axis=-1, keepdims=True)
    group_scale = lax.rsqrt(jnp.mean(centred * centred, axis=-1, keepdims=True) + norm_eps)
    unit_h = centred * group_scale
    gate_sig = jax.nn.sigmoid(gate)
    gate_act = gate * gate_sig
    gated = join_heads((gate_act * unit_h).astype(BF))
    branch = lax.psum_scatter(
        mm(gated, w_o).astype(BF), "sp", scatter_dimension=0, tiled=True
    ).astype(F32)
    hidden = own_x.astype(F32) + branch
    normed_b, unit_b, scale_b = layer_stats(hidden, gains[2], gains[3])
    b_low = lax.all_gather(perm(normed_b.astype(BF)), "sp", axis=0, tiled=True)
    up = mm(b_low, w_up)
    act_low = jax.nn.gelu(up, approximate=False).astype(BF)
    ffn = lax.psum_scatter(
        mm(act_low, w_down).astype(BF), "sp", scatter_dimension=0, tiled=True
    ).astype(F32)
    block_out = (hidden + ffn).astype(BF).reshape(block_input.shape)

    grad_top = grad_ffn_own.astype(F32)
    grad_act = mm_t(grad_ffn, w_down)
    density = (
        0.5 * (1.0 + lax.erf(up * root_half)) + up * jnp.exp(-0.5 * up * up) * inv_root_tau
    )
    grad_up = (grad_act * density).astype(BF)
    grad_b = unperm(
        lax.psum_scatter(
            mm_t(grad_up, w_up).astype(BF), "sp", scatter_dimension=0, tiled=True
        ).astype(F32)
    )
    grad_hidden = grad_top + layer_back(grad_b, unit_b, scale_b, gains[2])
    grad_branch = lax.all_gather(grad_hidden.astype(BF), "sp", axis=0, tiled=True)

    def reduce_rows(v):
        return lax.psum_scatter(v.astype(BF), PLANE, scatter_dimension=0, tiled=True)

    sum_down = reduce_rows(mm_tn(act_low, grad_ffn))
    sum_up = reduce_rows(mm_tn(b_low, grad_up))
    sum_o = reduce_rows(mm_tn(gated, grad_branch))

    grad_gated = split_heads(mm_t(grad_branch, w_o), DV)
    grad_gate = (grad_gated * unit_h * gate_sig * (1.0 + gate * (1.0 - gate_sig))).astype(BF)
    grad_unit = grad_gated * gate_act
    grad_mixed = (
        group_scale
        * (
            grad_unit
            - jnp.mean(grad_unit, axis=-1, keepdims=True)
            - unit_h * jnp.mean(grad_unit * unit_h, axis=-1, keepdims=True)
        )
    ).astype(BF)
    grad_read = (grad_mixed * inward).astype(BF)
    own_reach = ein("hik,hiv->hkv", qs, grad_read)
    reaches = lax.all_gather(own_reach.astype(BF), "ctx").astype(F32)
    reach = jnp.sum(reaches * fore_w[:, :, None, None], 0).astype(BF)
    grad_probs = ein("hiv,hjv->hij", grad_mixed, vs)
    grad_scores = (grad_probs * mask).astype(BF)
    grad_q = ein("hij,hjk->hik", grad_scores, ks) + ein("hiv,hkv->hik", grad_read, state)
    grad_k = ein("hij,hik->hjk", grad_scores, qs) + ein("hjv,hkv->hjk", vs, reach) * outward
    grad_v = ein("hij,hiv->hjv", probs, grad_mixed) + ein("hjk,hkv->hjv", key_decayed, reach)
    grad_proj = jnp.concatenate(
        [
            join_heads(rotate(grad_q, cos_h, sin_h, -1.0).astype(BF)),
            join_heads(rotate(grad_k, cos_h, sin_h, -1.0).astype(BF)),
            join_heads(grad_v.astype(BF)),
            join_heads(grad_gate),
        ],
        1,
    )
    grad_a = unperm(
        lax.psum_scatter(
            mm_t(grad_proj, w_proj).astype(BF), "sp", scatter_dimension=0, tiled=True
        ).astype(F32)
    )
    sum_proj = reduce_rows(mm_tn(a_low, grad_proj))
    _, unit_a, scale_a = layer_stats(own_x.astype(F32), gains[0], gains[1])
    grad_rows = grad_hidden + layer_back(grad_a, unit_a, scale_a, gains[0])
    grad_x = grad_rows.astype(BF).reshape(block_input.shape)
    norm_terms = jnp.stack(
        [
            jnp.sum(grad_a * unit_a, 0),
            jnp.sum(grad_a, 0),
            jnp.sum(grad_b * unit_b, 0),
            jnp.sum(grad_b, 0),
        ]
    )
    grad_gains = lax.psum_scatter(norm_terms, ALL, scatter_dimension=1, tiled=True)

    def home(v):
        v = v.reshape(sp_n, rows_in, -1)
        return lax.all_to_all(v, "sp", split_axis=0, concat_axis=0, tiled=True)

    back_proj = home(sum_proj)
    back_up = home(sum_up)
    edges = (0, qk_w, 2 * qk_w, 2 * qk_w + vd_w, cut)
    parts = [back_proj[:, :, a:b] for a, b in zip(edges[:-1], edges[1:])] + [back_up]
    grad_first = jnp.concatenate(
        [p.swapaxes(0, 1).reshape(rows_in, -1) for p in parts], 1
    ).astype(F32)
    grad_second = jnp.concatenate([sum_o, sum_down], 1).astype(F32)
    first_m, first_v, first_step = adam_update(weight_in, grad_first, moment_in, square_in)
    second_m, second_v, second_step = adam_update(weight_out, grad_second, moment_out, square_out)
    gain_m, gain_v, gain_step = adam_update(norm_gains, grad_gains, moment_norm, square_norm)
    return (
        block_out,
        grad_x,
        grad_first,
        first_m,
        first_v,
        first_step,
        grad_second,
        second_m,
        second_v,
        second_step,
        grad_gains,
        gain_m,
        gain_v,
        gain_step,
    )


def solution(mesh):
    tokens = P("fsdp", "ctx", "sp", None)
    rows = P(ALL, None)
    cols = P(None, ALL)
    in_specs = (tokens, tokens, P(), rows, rows, cols, rows, rows, rows, rows, cols, cols)
    out_specs = (tokens, tokens) + (rows,) * 8 + (cols,) * 4
    return jax.shard_map(shards, mesh=mesh, in_specs=in_specs, out_specs=out_specs, check_vma=False)
```

time: 3240 us -> 1160 us (0.36)
  waiting for transfers between devices: 2570 us -> 856 us
  other arithmetic: 196 us -> 53.2 us
  matrix products: 207 us -> 103 us
  blocking collectives: 142 us -> 47 us
    unnamed x9 -> x20, waiting for transfers between devices: 1390 us -> 134 us
    reduce_scatter x1 -> x8, waiting for transfers between devices: 630 us -> 341 us  [the longest x4 187 us: reduce_rows(): lax.psum_scatter(v.astype(BF), PLANE, scatter_dimension=0, tiled=True)]
    all_gather x4 -> x10, waiting for transfers between devices: 488 us -> 298 us  [the longest x1 48.4 us: shards(): b_low = lax.all_gather(perm(normed_b.astype(BF)), 'sp', axis=0, tiled=True)]
    concatenate x6 -> x0, other arithmetic: 135 us -> none  [the longest x1 88.2 us: shards(): jnp.concatenate([lax.dot_general(a_low, grad_proj, first_first, preferred...]
    dot_general x24, matrix products: 207 us -> 103 us  [the longest x4 32.7 us: mm(): return jnp.dot(a, b, preferred_element_type=F32)]
    all_to_all x2 -> x0, blocking collectives: 78.7 us -> none  [the longest x1 49.9 us: shards(): lax.all_to_all(out_pieces, 'sp', split_axis=0, concat_axis=1, tiled=True)]
    all_to_all x6 -> x3, waiting for transfers between devices: 61.6 us -> 83.2 us  [the longest x1 69.5 us: shards(): lax.all_to_all(slabs.swapaxes(0, 1), 'sp', split_axis=0, concat_axis=0, t...]
  transfers between devices with their start and end apart: 13 -> 22, of which waited for: 11 -> 20; matrix products, arithmetic and copies ran while one was open for 10% -> 12% of each run, Pallas kernels for 0% -> 0%
where the time goes in v1:
time: 1160 us
  waiting for transfers between devices  856 us (74%)
  matrix products  103 us (9%)
  local copies, waits for them, and re-layouts  66.6 us (6%)
  other arithmetic  53.2 us (5%)
  blocking collectives  47 us (4%)
  starting transfers between devices  17.7 us (2%)
  between operations  15.2 us (1%)
    reduce_scatter x4, waiting for transfers between devices, reduce_rows(): lax.psum_scatter(v.astype(BF), PLANE, scatter_dimension=0, tiled=True)  187 us
    unnamed x20, waiting for transfers between devices  134 us
    all_to_all x1, waiting for transfers between devices, shards(): lax.all_to_all(slabs.swapaxes(0, 1), 'sp', split_axis=0, concat_axis=0, t...  69.5 us
    all_gather x1, waiting for transfers between devices, shards(): b_low = lax.all_gather(perm(normed_b.astype(BF)), 'sp', axis=0, tiled=True)  48.4 us
    all_gather x1, blocking collectives, shards(): lax.all_gather(norm_gains.astype(BF), ALL, axis=1, tiled=True).astype(F32)  47 us
    all_gather x1, waiting for transfers between devices, shards(): lax.all_gather(grad_hidden.astype(BF), 'sp', axis=0, tiled=True)  44.8 us
    reduce_scatter x1, waiting for transfers between devices, shards(): lax.psum_scatter(mm(gated, w_o).astype(BF), 'sp', scatter_dimension=0, ti...  41.7 us
    reduce_scatter x1, waiting for transfers between devices, shards(): lax.psum_scatter(mm_t(grad_proj, w_proj).astype(BF), 'sp', scatter_dimens...  40 us
  transfers between devices with their start and end apart: 22, of which 20 were waited for; matrix products, arithmetic and copies ran while one was open for 12% of the time, Pallas kernels for 0%

profile of v1, /device:TPU:0, one launch (start us, length us, event | category | flops | bytes accessed | tf_op | source)
XLA Modules:
  0.0 1159.0 jit_solution(12375904361449977612)
XLA Ops:
  20.1 6.5 all-to-all-start
  27.9 69.5 %all-to-all-done = bf16[4,64,4096]{2,1,0:T(8,128)(2,1)S(1)} async-done(((bf16[4,64,4096]{2,1,0:T(8,128)(2,1)}), bf16[4,64,4096]{2,1,0:T(8,128)(2,1)S(1)}, u32[]{:S(2)}, u32[]{:S(2)}) %all-to-all-start) | async-done | bytes 2097184 | tf_op jit(solution)/shard_map/all_to_all | solution.py:135
  99.2 47.0 %all-gather.3 = bf16[32,64,4]{1,2,0:T(4,128)(2,1)S(1)} all-gather(bf16[1,64,4]{1,2,0:T(4,128)(2,1)S(1)} %convert_bitcast_fusion.1), channel_id=1, replica_groups=mesh['sp'=4,'ctx'=4,'fsdp'=2] {'sp','ctx','fsdp'}, dimensions={0}, use_global_device_ids=true | all-gather | bytes 16896 | tf_op jit(solution)/shard_map/all_gather | solution.py:142
  150.7 33.3 %all-gather.17.cloned.1.call-done = bf16[2048,3072]{1,0:T(8,128)(2,1)} async-done(((bf16[256,3072]{1,0:T(8,128)(2,1)}), bf16[2048,3072]{1,0:T(8,128)(2,1)}) %all-gather.17.cloned.1.call-update) | async-done | bytes 12582928 | tf_op jit(solution)/shard_map/all_gather | solution.py:137
  184.1 10.3 fusion.74
  216.8 21.5 %all-gather.29.cloned.1.call-done = bf16[8,256,512]{2,1,0:T(8,128)(2,1)} async-done(((bf16[2,256,512]{2,1,0:T(8,128)(2,1)}), bf16[8,256,512]{2,1,0:T(8,128)(2,1)}) %all-gather.29.cloned.1.call-update) | async-done | bytes 2097168 | tf_op jit(solution)/shard_map/all_gather | solution.py:191
  246.5 30.8 %all-gather.19.cloned.1.call-done = bf16[1024,2048]{1,0:T(8,128)(2,1)} async-done(((bf16[128,2048]{1,0:T(8,128)(2,1)}), bf16[1024,2048]{1,0:T(8,128)(2,1)}) %all-gather.19.cloned.1.call-update) | async-done | bytes 4194320 | tf_op jit(solution)/shard_map/all_gather | solution.py:140
  277.3 6.2 convolution_convert_fusion.7
  285.6 41.7 %reduce-scatter.12.cloned.1.call-done = bf16[128,2048]{1,0:T(8,128)(2,1)} async-done(((bf16[512,2048]{1,0:T(8,128)(2,1)}), bf16[128,2048]{1,0:T(8,128)(2,1)}) %reduce-scatter.12.cloned.1.call-update) | async-done | bytes 524304 | tf_op jit(solution)/shard_map/reduce_scatter | solution.py:203
  337.0 28.4 %all-gather.23.cloned.1.call-done = bf16[2048,1024]{1,0:T(8,128)(2,1)} async-done(((bf16[256,1024]{1,0:T(8,128)(2,1)}), bf16[2048,1024]{1,0:T(8,128)(2,1)}) %all-gather.23.cloned.1.call-update) | async-done | bytes 4194320 | tf_op jit(solution)/shard_map/all_gather | solution.py:138
  365.4 48.4 %all-gather.21.cloned.1.call-done = bf16[512,2048]{0,1:T(8,128)(2,1)} async-done(((bf16[128,2048]{0,1:T(8,128)(2,1)}), bf16[512,2048]{0,1:T(8,128)(2,1)}) %all-gather.21.cloned.1.call-update) | async-done | bytes 2097168 | tf_op jit(solution)/shard_map/all_gather | solution.py:208
  413.9 10.0 fusion.20
  423.9 35.5 %all-gather.31.cloned.1.call-done = bf16[1,1,512,2048]{3,2,1,0:T(8,128)(2,1)} async-done(((bf16[1,1,128,2048]{3,2,1,0:T(8,128)(2,1)}), bf16[1,1,512,2048]{3,2,1,0:T(8,128)(2,1)}) %all-gather.31.cloned.1.call-update) | async-done | bytes 2097168 | tf_op jit(solution)/shard_map/all_gather | solution.py:149
  459.4 37.8 %all-gather.25.cloned.1.call-done = bf16[1024,2048]{1,0:T(8,128)(2,1)} async-done(((bf16[128,2048]{1,0:T(8,128)(2,1)}), bf16[1024,2048]{1,0:T(8,128)(2,1)}) %all-gather.25.cloned.1.call-update) | async-done | bytes 4194320 | tf_op jit(solution)/shard_map/all_gather | solution.py:141
  497.2 6.4 fusion.26
  508.4 6.2 convolution_convert_fusion.6
  514.9 37.3 %reduce-scatter.16.cloned.1.call-done = bf16[128,2048]{1,0:T(8,128)(2,1)} async-done(((bf16[512,2048]{1,0:T(8,128)(2,1)}), bf16[128,2048]{1,0:T(8,128)(2,1)}) %reduce-scatter.16.cloned.1.call-update) | async-done | bytes 524304 | tf_op jit(solution)/shard_map/reduce_scatter | solution.py:223
  562.8 35.1 %reduce-scatter.14.cloned.1.call-done = bf16[128,2048]{1,0:T(8,128)(2,1)} async-done(((bf16[512,2048]{1,0:T(8,128)(2,1)}), bf16[128,2048]{1,0:T(8,128)(2,1)}) %reduce-scatter.14.cloned.1.call-update) | async-done | bytes 524304 | tf_op jit(solution)/shard_map/reduce_scatter | solution.py:211
  601.7 44.8 %all-gather.27.cloned.1.call-done = bf16[512,2048]{1,0:T(8,128)(2,1)} async-done(((bf16[128,2048]{1,0:T(8,128)(2,1)}), bf16[512,2048]{1,0:T(8,128)(2,1)}) %all-gather.27.cloned.1.call-update) | async-done | bytes 2097168 | tf_op jit(solution)/shard_map/all_gather | solution.py:228
  656.1 6.2 convolution_convert_fusion.3
  672.4 17.8 %all-gather.33.cloned.1.call-done = bf16[8,256,512]{2,1,0:T(8,128)(2,1)} async-done(((bf16[2,256,512]{2,1,0:T(8,128)(2,1)}), bf16[8,256,512]{2,1,0:T(8,128)(2,1)}) %all-gather.33.cloned.1.call-update) | async-done | bytes 2097168 | tf_op jit(solution)/shard_map/all_gather | solution.py:250
  702.5 9.7 convolution_convert_fusion
  728.3 10.8 convolution_convert_fusion.4
  739.1 6.0 reduce-scatter.22.cloned.1.call-done
  750.3 13.8 %all-to-all-done.2 = bf16[4,64,1024]{2,1,0:T(8,128)(2,1)S(1)} async-done(((bf16[4,64,1024]{2,1,0:T(8,128)(2,1)}), bf16[4,64,1024]{2,1,0:T(8,128)(2,1)S(1)}, u32[]{:S(2)}, u32[]{:S(2)}) %all-to-all-start.2) | async-done | bytes 524320 | tf_op jit(solution)/shard_map/all_to_all | solution.py:287
  764.9 75.9 %reduce-scatter.20.cloned.1.call-done = bf16[256,3072]{1,0:T(8,128)(2,1)} async-done(((bf16[2048,3072]{1,0:T(8,128)(2,1)}), bf16[256,3072]{1,0:T(8,128)(2,1)}) %reduce-scatter.20.cloned.1.call-update) | async-done | bytes 1572880 | tf_op jit(solution)/shard_map/reduce_scatter | solution.py:231
  845.7 50.1 %reduce-scatter.26.cloned.1.call-done = bf16[128,2048]{1,0:T(8,128)(2,1)} async-done(((bf16[1024,2048]{1,0:T(8,128)(2,1)}), bf16[128,2048]{1,0:T(8,128)(2,1)}) %reduce-scatter.26.cloned.1.call-update) | async-done | bytes 524304 | tf_op jit(solution)/shard_map/reduce_scatter | solution.py:231
  895.8 55.0 %reduce-scatter.24.cloned.1.call-done = bf16[128,2048]{1,0:T(8,128)(2,1)} async-done(((bf16[1024,2048]{1,0:T(8,128)(2,1)}), bf16[128,2048]{1,0:T(8,128)(2,1)}) %reduce-scatter.24.cloned.1.call-update) | async-done | bytes 524304 | tf_op jit(solution)/shard_map/reduce_scatter | solution.py:231
  950.7 6.4 add_multiply_fusion.1
  957.1 40.0 %reduce-scatter.18.cloned.1.call-done = bf16[128,2048]{1,0:T(8,128)(2,1)} async-done(((bf16[512,2048]{1,0:T(8,128)(2,1)}), bf16[128,2048]{1,0:T(8,128)(2,1)}) %reduce-scatter.18.cloned.1.call-update) | async-done | bytes 524304 | tf_op jit(solution)/shard_map/reduce_scatter | solution.py:267
  1004.8 132.1 %reduce-scatter.28.cloned.1.call-done = f32[64,4]{1,0:T(8,128)} async-done(((f32[2048,4]{1,0:T(8,128)}), f32[64,4]{1,0:T(8,128)}) %reduce-scatter.28.cloned.1.call-update) | async-done | bytes 1040
  1143.6 8.6 add_multiply_fusion
  (299 shorter events, 154.7 us)
Async XLA Ops:
  20.1 77.2 %all-to-all-start = ((bf16[4,64,4096]{2,1,0:T(8,128)(2,1)}), bf16[4,64,4096]{2,1,0:T(8,128)(2,1)S(1)}, u32[]{:S(2)}, u32[]{:S(2)}) async-start(bf16[4,64,4096]{2,1,0:T(8,128)(2,1)} %copy.245), calls=%async_computation | async-start | bytes 4194304 | tf_op jit(solution)/shard_map/all_to_all | solution.py:135
  26.6 121.2 %all-gather.15.cloned.1.call-start = ((), (), s32[]{:S(2)}) async-start(), calls=%async_computation.12 | async-start | bytes 2621440 | tf_op jit(solution)/shard_map/all_gather | solution.py:148
  26.8 71.8 %copy-start.18 = (bf16[1,1,128,2048]{2,3,1,0:T(8,128)(2,1)}, bf16[1,1,128,2048]{2,3,1,0:T(8,128)(2,1)S(1)}, u32[]{:S(2)}) copy-start(bf16[1,1,128,2048]{2,3,1,0:T(8,128)(2,1)S(1)} %copy.241) | copy-start | bytes 1572868
  27.8 156.3 %all-gather.17.cloned.1.call-start = ((), (), s32[]{:S(2)}) async-start(), calls=%async_computation.13 | async-start | bytes 14155776 | tf_op jit(solution)/shard_map/all_gather | solution.py:137
  97.3 49.3 %copy-start.58 = (f32[8]{0:T(128)S(1)}, f32[8]{0:T(128)}, u32[]{:S(2)}) copy-start(f32[8]{0:T(128)} %param.14) | copy-start | bytes 100
  99.1 139.2 %all-gather.29.cloned.1.call-start = ((), (), s32[]{:S(2)}) async-start(), calls=%async_computation.27 | async-start | bytes 2621440 | tf_op jit(solution)/shard_map/all_gather | solution.py:191
  147.8 52.6 %copy-start.30 = (f32[512,128]{1,0:T(8,128)}, f32[512,128]{1,0:T(8,128)S(1)}, u32[]{:S(2)}) copy-start(f32[512,128]{1,0:T(8,128)S(1)} %get-tuple-element.81) | copy-start | bytes 786436
  203.0 74.3 %all-gather.19.cloned.1.call-start = ((), (), s32[]{:S(2)}) async-start(), calls=%async_computation.14 | async-start | bytes 4718592 | tf_op jit(solution)/shard_map/all_gather | solution.py:140
  205.9 121.4 %reduce-scatter.12.cloned.1.call-start = ((), (), s32[]{:S(2)}) async-start(), calls=%async_computation.15 | async-start | bytes 2621440 | tf_op jit(solution)/shard_map/reduce_scatter | solution.py:203
  216.8 23.6 %copy-start.38 = (bf16[2,512,128]{2,1,0:T(8,128)(2,1)S(1)}, bf16[2,512,128]{2,1,0:T(8,128)(2,1)}, u32[]{:S(2)}) copy-start(bf16[2,512,128]{2,1,0:T(8,128)(2,1)} %get-tuple-element.60) | copy-start | bytes 786436
  216.8 23.7 %copy-start.41 = (bf16[2,512,128]{2,1,0:T(8,128)(2,1)S(1)}, bf16[2,512,128]{2,1,0:T(8,128)(2,1)}, u32[]{:S(2)}) copy-start(bf16[2,512,128]{2,1,0:T(8,128)(2,1)} %get-tuple-element.61) | copy-start | bytes 786436
  283.5 81.9 %all-gather.23.cloned.1.call-start = ((), (), s32[]{:S(2)}) async-start(), calls=%async_computation.17 | async-start | bytes 4718592 | tf_op jit(solution)/shard_map/all_gather | solution.py:138
  285.5 128.4 %all-gather.21.cloned.1.call-start = ((), (), s32[]{:S(2)}) async-start(), calls=%async_computation.16 | async-start | bytes 2621440 | tf_op jit(solution)/shard_map/all_gather | solution.py:208
  335.0 124.4 %all-gather.31.cloned.1.call-start = ((), (), s32[]{:S(2)}) async-start(), calls=%async_computation.28 | async-start | bytes 2621440 | tf_op jit(solution)/shard_map/all_gather | solution.py:149
  335.8 161.4 %all-gather.25.cloned.1.call-start = ((), (), s32[]{:S(2)}) async-start(), calls=%async_computation.18 | async-start | bytes 4718592 | tf_op jit(solution)/shard_map/all_gather | solution.py:141
  336.5 215.6 %reduce-scatter.16.cloned.1.call-start = ((), (), s32[]{:S(2)}) async-start(), calls=%async_computation.20 | async-start | bytes 2621440 | tf_op jit(solution)/shard_map/reduce_scatter | solution.py:223
  508.4 89.5 %reduce-scatter.14.cloned.1.call-start = ((), (), s32[]{:S(2)}) async-start(), calls=%async_computation.19 | async-start | bytes 2621440 | tf_op jit(solution)/shard_map/reduce_scatter | solution.py:211
  514.6 131.9 %all-gather.27.cloned.1.call-start = ((), (), s32[]{:S(2)}) async-start(), calls=%async_computation.21 | async-start | bytes 2621440 | tf_op jit(solution)/shard_map/all_gather | solution.py:228
  601.5 88.7 %all-gather.33.cloned.1.call-start = ((), (), s32[]{:S(2)}) async-start(), calls=%async_computation.29 | async-start | bytes 2621440 | tf_op jit(solution)/shard_map/all_gather | solution.py:250
  656.0 89.1 %reduce-scatter.22.cloned.1.call-start = ((), (), s32[]{:S(2)}) async-start(), calls=%async_computation.24 | async-start | bytes 4718592 | tf_op jit(solution)/shard_map/reduce_scatter | solution.py:231
  662.3 178.5 %reduce-scatter.20.cloned.1.call-start = ((), (), s32[]{:S(2)}) async-start(), calls=%async_computation.23 | async-start | bytes 14155776 | tf_op jit(solution)/shard_map/reduce_scatter | solution.py:231
  672.4 19.9 %copy-start.29 = (f32[2,512,256]{2,1,0:T(8,128)S(1)}, f32[2,512,256]{2,1,0:T(8,128)}, u32[]{:S(2)}) copy-start(f32[2,512,256]{2,1,0:T(8,128)} %fusion.72) | copy-start | bytes 3145732
  712.2 183.5 %reduce-scatter.26.cloned.1.call-start = ((), (), s32[]{:S(2)}) async-start(), calls=%async_computation.26 | async-start | bytes 4718592 | tf_op jit(solution)/shard_map/reduce_scatter | solution.py:231
  719.4 231.3 %reduce-scatter.24.cloned.1.call-start = ((), (), s32[]{:S(2)}) async-start(), calls=%async_computation.25 | async-start | bytes 4718592 | tf_op jit(solution)/shard_map/reduce_scatter | solution.py:231
  726.6 270.5 %reduce-scatter.18.cloned.1.call-start = ((), (), s32[]{:S(2)}) async-start(), calls=%async_computation.22 | async-start | bytes 2621440 | tf_op jit(solution)/shard_map/reduce_scatter | solution.py:267
  745.1 18.9 %all-to-all-start.2 = ((bf16[4,64,1024]{2,1,0:T(8,128)(2,1)}), bf16[4,64,1024]{2,1,0:T(8,128)(2,1)S(1)}, u32[]{:S(2)}, u32[]{:S(2)}) async-start(bf16[4,64,1024]{2,1,0:T(8,128)(2,1)} %bitcast.244), calls=%async_computation.8 | async-start | bytes 1048576 | tf_op jit(solution)/shard_map/all_to_all | solution.py:287
  764.1 186.7 %copy-start.12 = (f32[128,4096]{1,0:T(8,128)S(1)}, f32[128,4096]{1,0:T(8,128)}, u32[]{:S(2)}) copy-start(f32[128,4096]{1,0:T(8,128)} %param.16) | copy-start | bytes 6291460
  840.8 297.5 %all-to-all-start.1 = ((bf16[4,64,3072]{2,1,0:T(8,128)(2,1)}), bf16[4,64,3072]{2,1,0:T(8,128)(2,1)}, u32[]{:S(2)}, u32[]{:S(2)}) async-start(bf16[4,64,3072]{2,1,0:T(8,128)(2,1)} %bitcast.235), calls=%async_computation.6 | async-start | bytes 3145728 | tf_op jit(solution)/shard_map/all_to_all | solution.py:287
  845.4 291.4 %reduce-scatter.28.cloned.1.call-start = ((), (), s32[]{:S(2)}) async-start(), calls=%async_computation.30 | async-start | bytes 1081344
  957.1 41.3 %copy-start.19 = (bf16[1,1,128,2048]{2,3,1,0:T(8,128)(2,1)S(1)}, bf16[1,1,128,2048]{2,3,1,0:T(8,128)(2,1)}, u32[]{:S(2)}) copy-start(bf16[1,1,128,2048]{2,3,1,0:T(8,128)(2,1)} %copy-done.18) | copy-start | bytes 1572868
  1002.3 135.4 %copy-start.56 = (f32[4,64]{1,0:T(4,128)S(1)}, f32[4,64]{1,0:T(4,128)}, u32[]{:S(2)}) copy-start(f32[4,64]{1,0:T(4,128)} %param.23) | copy-start | bytes 3076
  1002.3 135.4 %copy-start.57 = (f32[4,64]{1,0:T(4,128)S(1)}, f32[4,64]{1,0:T(4,128)}, u32[]{:S(2)}) copy-start(f32[4,64]{1,0:T(4,128)} %param.22) | copy-start | bytes 3076
  (52 other events, 156.5 us)
Sparse Core Ops, SparseCore 0:
  29.5 81.7 all-gather.14
  113.7 70.2 all-gather.16
  203.2 35.1 all-gather.28
  240.7 36.5 all-gather.18
  283.6 43.6 reduce-scatter.11
  329.6 35.7 all-gather.22
  367.6 46.2 all-gather.20
  415.4 43.9 all-gather.30
  461.9 35.2 all-gather.24
  508.5 43.6 reduce-scatter.15
  555.0 42.8 reduce-scatter.13
  601.6 44.8 all-gather.26
  656.2 33.9 all-gather.32
  694.0 51.1 reduce-scatter.21
  748.5 92.2 reduce-scatter.19
  844.6 51.1 reduce-scatter.25
  899.5 51.1 reduce-scatter.23
  953.4 43.6 reduce-scatter.17
  1001.1 135.7 reduce-scatter.27
